TPU v7x, 32 devices: a whole 2x2x4 slice. The times are simulated.
32 devices in a mesh: prow: 4 (over y, x), pcol: 8 (over z, core).
Axes of the slice: x: 2, y: 2, z: 4, core: 2. Of those that a mesh axis runs over, the one named last changes fastest.
Arguments:
- matrix: float32 [16, 4, 256, 8, 8, 256], P(None, 'prow', None, None, 'pcol'), may hold values from -6 to 6, as said below
- factor: float32 [16, 4, 256, 8, 8, 256], P(None, 'prow', None, None, 'pcol'), may hold values from -3 to 3, as said below
Outputs:
- reduced: float32 [16, 4, 256, 8, 8, 256], P(None, 'prow', None, None, 'pcol')
Inputs may be any that keep to these rules, and one draw needn't show every extreme that they name: Symmetric matrix stored in its lower triangle: every entry above the diagonal is zero. `factor`: lower triangular with diagonal entries between 1 and 3; every entry above the diagonal is zero.
All inputs are finite; a program needn't handle non-finite values.
Results may differ from a plain program's by a relative error of at most 0.0001.
Values sent between devices are 32-bit elements; how exact they have to be, the bound alone decides.
A program may use at most 256 MiB of HBM per device.

v0:
```python
import jax
import jax.numpy as jnp
from jax import lax
from jax.sharding import PartitionSpec as P

BLOCKS = 2


highest = lax.Precision.HIGHEST


def spread(block, axis, source):
    block = jnp.where(lax.axis_index(axis) == source, block, jnp.zeros_like(block))
    return lax.psum(block, axis)


def product(left, right):
    return jnp.dot(left, right, precision=highest, preferred_element_type=jnp.float32)


def product_trans(left, right):
    return lax.dot_general(
        left, right, (((1,), (1,)), ((), ())), precision=highest, preferred_element_type=jnp.float32
    )


def diagonal_core(diag_block, diag_factor, width):
    identity = jnp.eye(width, dtype=jnp.float32)
    inverse = lax.linalg.triangular_solve(diag_factor, identity, left_side=True, lower=True)
    symmetric = diag_block + diag_block.T - jnp.diag(jnp.diagonal(diag_block))
    inner = product_trans(product(inverse, symmetric), inverse)
    return (inverse, 0.5 * (inner + inner.T))


def on_device(matrix, factor):
    row_tiles = matrix.shape[0]
    width = matrix.shape[2]
    col_tiles = matrix.shape[3]
    prow_count = lax.axis_size("prow")
    pcol_count = lax.axis_size("pcol")
    prow_index = lax.axis_index("prow")
    pcol_index = lax.axis_index("pcol")
    height = row_tiles * width
    local = matrix.reshape(height, col_tiles * width)
    factor_local = factor.reshape(height, col_tiles * width)
    tile_rows = jnp.arange(row_tiles, dtype=jnp.int32) * prow_count + prow_index
    tile_cols = jnp.arange(col_tiles, dtype=jnp.int32) * pcol_count + pcol_index
    offsets = jnp.arange(width, dtype=jnp.int32)
    elem_rows = (tile_rows[:, None] * width + offsets[None, :]).reshape(height)
    elem_cols = (tile_cols[:, None] * width + offsets[None, :]).reshape(col_tiles * width)
    lower_part = elem_rows[:, None] >= elem_cols[None, :]
    row_tile_of = jnp.repeat(tile_rows, width)[:, None]
    ratio = pcol_count // prow_count
    home = pcol_index % prow_count

    def select_columns(block):
        shaped = block.reshape(col_tiles, ratio, width, width)
        picked = lax.dynamic_index_in_dim(shaped, pcol_index // prow_count, 1, keepdims=False)
        return picked.reshape(col_tiles * width, width)

    for step in range(BLOCKS):
        owner_row = step % prow_count
        owner_col = step % pcol_count
        first = step // pcol_count * width
        diag_start = step // prow_count * width
        panel = local[:, first : first + width]
        factor_panel = factor_local[:, first : first + width]
        diag_block, diag_factor = (
            spread(panel[diag_start : diag_start + width], "prow", owner_row),
            spread(factor_panel[diag_start : diag_start + width], "prow", owner_row),
        )
        inverse, core = diagonal_core(diag_block, diag_factor, width)
        below = row_tile_of > step
        factor_rows = jnp.where(below, factor_panel, 0.0)
        shared = product(factor_rows, core)
        halfway = jnp.where(below, product_trans(panel, inverse), 0.0) - 0.5 * shared
        finished = halfway - 0.5 * shared
        got_half, got_factor = (
            spread(halfway, "pcol", owner_col),
            spread(factor_rows, "pcol", owner_col),
        )
        keeper = prow_index == home
        col_half, col_factor = lax.psum(
            (
                jnp.where(keeper, select_columns(got_half), 0.0),
                jnp.where(keeper, select_columns(got_factor), 0.0),
            ),
            "prow",
        )
        update = product_trans(
            jnp.concatenate([got_half, got_factor], 1), jnp.concatenate([col_factor, col_half], 1)
        )
        local = local - jnp.where(lower_part, update, 0.0)
        current = local[:, first : first + width]
        diag_rows = jnp.tile(jnp.tril(core), (row_tiles, 1))
        column = jnp.where(row_tile_of == step, diag_rows, jnp.where(below, finished, current))
        column = jnp.where(pcol_index == owner_col, column, current)
        local = local.at[:, first : first + width].set(column)
    return local.reshape(row_tiles, 1, width, col_tiles, 1, width)


def solution(mesh):
    placed = (P(None, "prow", None, None, "pcol", None), P(None, "prow", None, None, "pcol", None))
    return jax.shard_map(
        on_device,
        mesh=mesh,
        in_specs=placed,
        out_specs=P(None, "prow", None, None, "pcol", None),
        check_vma=False,
    )
```

profile of v0, /device:TPU:0, one launch (start us, length us, event | category | flops | bytes accessed | tf_op | source)
XLA Modules:
  0.0 1339.8 jit_solution(16150928784970390900)
XLA Ops:
  6.5 94.1 %reduce.10 = f32[16,256,8,256]{3,2,1,0:T(8,128)} reduce(f32[16,1,256,8,1,256]{5,4,3,2,1,0:T(1,128)} %param.8, f32[]{:T(128)} %constant.182), dimensions={1,4}, to_apply=%param.8.reduce_sub_computation | reduce | bytes 67108864 | tf_op args[0]
  100.6 29.9 %copy.42 = f32[512,8,8,256]{3,1,2,0:T(8,128)} copy(f32[512,8,8,256]{3,2,1,0:T(8,128)} %bitcast.119) | data formatting | bytes 67108864
  130.5 31.1 %copy.36 = f32[4096,2048]{0,1:T(8,128)} copy(f32[4096,2048]{1,0:T(8,128)} %bitcast.120) | data formatting | bytes 67108864 | tf_op jit(solution)/shard_map/reshape | solution.py:44
  161.6 93.3 %reduce.9 = f32[16,256,8,256]{3,2,1,0:T(8,128)} reduce(f32[16,1,256,8,1,256]{5,4,3,2,1,0:T(1,128)} %param.9, f32[]{:T(128)} %constant.182), dimensions={1,4}, to_apply=%param.9.reduce_sub_computation | reduce | bytes 67108864 | tf_op args[1]
  254.9 29.9 %copy.45 = f32[512,8,8,256]{3,1,2,0:T(8,128)} copy(f32[512,8,8,256]{3,2,1,0:T(8,128)} %bitcast.118) | data formatting | bytes 67108864
  285.9 1.9 broadcast_select_fusion.6
  287.8 4.5 slice.126
  292.4 5.9 copy.41
  298.4 6.9 select_select_fusion.2
  305.4 30.7 %all-reduce.23.cloned.1.call-done = (f32[256,256]{0,1:T(8,128)}, f32[256,256]{0,1:T(8,128)}) async-done(((f32[256,256]{0,1:T(8,128)}, f32[256,256]{0,1:T(8,128)}), (f32[256,256]{0,1:T(8,128)}, f32[256,256]{0,1:T(8,128)})) %all-reduce.23.cloned.1.call-update) | async-done | bytes 524304 | tf_op jit(solution)/shard_map/psum | solution.py:14
  338.3 4.2 while.6
  338.9 1.4 dynamic-slice.28
  341.0 1.4 dynamic-slice.28
  342.5 19.7 %custom-call.8 = f32[2,128,128]{1,2,0:T(8,128)S(1)} custom-call(f32[2,128,128]{2,1,0:T(8,128)S(1)} %get-tuple-element.44), custom_call_target="InvertDiagBlocksLowerTriangular" | custom-call | tf_op jit(solution)/shard_map/triangular_solve/custom-call.1 | solution.py:29
  363.2 2.4 gather_fusion
  366.6 5.9 convolution_multiply_fusion.1
  372.5 10.7 broadcast_select_fusion.5
  383.3 175.6 %all-reduce.15.cloned.1.call-done = (f32[4096,256]{0,1:T(8,128)}, f32[4096,256]{0,1:T(8,128)}) async-done(((f32[4096,256]{0,1:T(8,128)}, f32[4096,256]{0,1:T(8,128)}), (f32[4096,256]{0,1:T(8,128)}, f32[4096,256]{0,1:T(8,128)})) %all-reduce.15.cloned.1.call-update) | async-done | bytes 8388624 | tf_op jit(solution)/shard_map/psum | solution.py:14
  559.0 7.0 reshape.187
  566.0 8.3 fusion.22
  574.3 2.2 copy.47
  576.5 6.7 reshape.186
  583.2 8.3 fusion.21
  591.5 2.3 copy.46
  595.2 5.7 copy.48
  600.9 96.8 %all-reduce.21.cloned.1.call-done = (f32[2048,256]{0,1:T(8,128)}, f32[2048,256]{0,1:T(8,128)}) async-done(((f32[2048,256]{0,1:T(8,128)}, f32[2048,256]{0,1:T(8,128)}), (f32[2048,256]{0,1:T(8,128)}, f32[2048,256]{0,1:T(8,128)})) %all-reduce.21.cloned.1.call-update) | async-done | bytes 4194320 | tf_op jit(solution)/shard_map/psum | solution.py:83
  697.7 65.8 %fusion = f32[4096,2048]{0,1:T(8,128)} fusion(f32[4096,2048]{0,1:T(8,128)} %copy.36, s32[4096]{0:T(1024)S(1)} %bitcast.140, s32[2048]{0:T(1024)S(1)} %bitcast.138, f32[4096,256]{0,1:T(8,128)} %get-tuple-element.80, f32[4096,256]{0,1:T(8,128)} %get-tuple-element.81, f32[2048,256]{0,1:T(8,128)} %get-tuple-element.86, f32[2048,256]{0,1:T(8,128)} %get-tuple-element.87), kind=kOutput, calls=%fused_computation.8 | convolution fusion | flops 51567919104 | bytes 79716352 | tf_op jit(solution)/shard_map/dot_general | solution.py:22
  763.6 12.5 constant_dynamic-update-slice_fusion
  776.1 1.7 slice_select_fusion
  777.9 45.5 %all-reduce.19.cloned.1.call-done = (f32[256,256]{0,1:T(8,128)}, f32[256,256]{0,1:T(8,128)}) async-done(((f32[256,256]{0,1:T(8,128)}, f32[256,256]{0,1:T(8,128)}), (f32[256,256]{0,1:T(8,128)}, f32[256,256]{0,1:T(8,128)})) %all-reduce.19.cloned.1.call-update) | async-done | bytes 524304 | tf_op jit(solution)/shard_map/psum | solution.py:14
  824.5 2.6 gather_fusion.1
  828.1 4.6 while.7
  832.7 19.7 %custom-call.9 = f32[2,128,128]{1,2,0:T(8,128)S(1)} custom-call(f32[2,128,128]{2,1,0:T(8,128)S(1)} %get-tuple-element.45), custom_call_target="InvertDiagBlocksLowerTriangular" | custom-call | tf_op jit(solution)/shard_map/triangular_solve/custom-call.1 | solution.py:29
  854.5 6.0 convolution_multiply_fusion
  860.5 6.5 broadcast_select_fusion.4
  867.1 175.7 %all-reduce.13.cloned.1.call-done = (f32[4096,256]{0,1:T(8,128)}, f32[4096,256]{0,1:T(8,128)}) async-done(((f32[4096,256]{0,1:T(8,128)}, f32[4096,256]{0,1:T(8,128)}), (f32[4096,256]{0,1:T(8,128)}, f32[4096,256]{0,1:T(8,128)})) %all-reduce.13.cloned.1.call-update) | async-done | bytes 8388624 | tf_op jit(solution)/shard_map/psum | solution.py:14
  1042.7 6.7 reshape.189
  1049.5 8.3 fusion.24
  1057.8 2.2 copy.50
  1060.0 6.8 reshape.188
  1066.8 8.3 fusion.23
  1075.1 2.2 copy.49
  1077.8 5.9 copy.51
  1083.7 97.5 %all-reduce.17.cloned.1.call-done = (f32[2048,256]{0,1:T(8,128)}, f32[2048,256]{0,1:T(8,128)}) async-done(((f32[2048,256]{0,1:T(8,128)}, f32[2048,256]{0,1:T(8,128)}), (f32[2048,256]{0,1:T(8,128)}, f32[2048,256]{0,1:T(8,128)})) %all-reduce.17.cloned.1.call-update) | async-done | bytes 4194320 | tf_op jit(solution)/shard_map/psum | solution.py:83
  1181.2 66.0 %fusion.1 = f32[4096,2048]{0,1:T(8,128)} fusion(f32[4096,2048]{0,1:T(8,128)} %get-tuple-element.90, s32[4096]{0:T(1024)S(1)} %bitcast.141, s32[2048]{0:T(1024)S(1)} %bitcast.139, f32[4096,256]{0,1:T(8,128)} %get-tuple-element.78, f32[4096,256]{0,1:T(8,128)} %get-tuple-element.79, f32[2048,256]{0,1:T(8,128)} %get-tuple-element.82, ...), kind=kOutput, calls=%fused_computation.9 | convolution fusion | flops 51567919104 | bytes 79716352 | tf_op jit(solution)/shard_map/dot_general | solution.py:22
  1247.3 6.6 fusion.11
  1253.9 30.1 %copy.52 = f32[256,8,16,256]{3,2,1,0:T(8,128)} copy(f32[256,8,16,256]{3,1,2,0:T(8,128)} %bitcast.117) | data formatting | bytes 67108864
  1284.0 48.7 %copy.30 = f32[16,1,256,8,1,256]{5,4,3,2,1,0:T(1,128)} copy(f32[16,1,256,8,1,256]{2,0,5,3,4,1:T(8,128)} %bitcast.121) | data formatting | bytes 67108864 | tf_op jit(solution)/shard_map/reshape | solution.py:99
  (92 shorter events, 17.2 us)
Async XLA Ops:
  6.5 329.5 %all-reduce.23.cloned.1.call-start = ((), (), s32[]{:S(2)}) async-start(), calls=%async_computation.5 | async-start | bytes 1048576 | tf_op jit(solution)/shard_map/psum | solution.py:14
  287.8 271.2 %all-reduce.15.cloned.1.call-start = ((), (), s32[]{:S(2)}) async-start(), calls=%async_computation.1 | async-start | bytes 16777216 | tf_op jit(solution)/shard_map/psum | solution.py:14
  336.0 27.2 %copy-start.6 = (f32[256,256]{0,1:T(8,128)S(1)}, f32[256,256]{0,1:T(8,128)}, u32[]{:S(2)}) copy-start(f32[256,256]{0,1:T(8,128)} %get-tuple-element.88) | copy-start | bytes 786436
  372.5 10.8 copy-start.2
  383.3 314.5 %all-reduce.21.cloned.1.call-start = ((), (), s32[]{:S(2)}) async-start(), calls=%async_computation.4 | async-start | bytes 8388608 | tf_op jit(solution)/shard_map/psum | solution.py:83
  593.8 229.6 %all-reduce.19.cloned.1.call-start = ((), (), s32[]{:S(2)}) async-start(), calls=%async_computation.3 | async-start | bytes 1048576 | tf_op jit(solution)/shard_map/psum | solution.py:14
  777.8 264.9 %all-reduce.13.cloned.1.call-start = ((), (), s32[]{:S(2)}) async-start(), calls=%async_computation | async-start | bytes 16777216 | tf_op jit(solution)/shard_map/psum | solution.py:14
  823.4 30.1 %copy-start.7 = (f32[256,256]{0,1:T(8,128)S(1)}, f32[256,256]{0,1:T(8,128)}, u32[]{:S(2)}) copy-start(f32[256,256]{0,1:T(8,128)} %get-tuple-element.84) | copy-start | bytes 786436
  854.4 6.1 copy-start.3
  860.5 6.5 copy-start
  867.0 314.2 %all-reduce.17.cloned.1.call-start = ((), (), s32[]{:S(2)}) async-start(), calls=%async_computation.2 | async-start | bytes 8388608 | tf_op jit(solution)/shard_map/psum | solution.py:83
  1181.2 66.0 %copy-start.1 = (f32[4096,256]{0,1:T(8,128)S(1)}, f32[4096,256]{0,1:T(8,128)}, u32[]{:S(2)}) copy-start(f32[4096,256]{0,1:T(8,128)} %copy-done) | copy-start | bytes 12582916
  1181.2 66.0 %copy-start.4 = (f32[32,8,16,256]{3,1,2,0:T(8,128)S(1)}, f32[32,8,16,256]{3,1,2,0:T(8,128)}, u32[]{:S(2)}) copy-start(f32[32,8,16,256]{3,1,2,0:T(8,128)} %copy.51) | copy-start | bytes 12582916
  1181.2 66.0 %copy-start.5 = (f32[4096,256]{0,1:T(8,128)S(1)}, f32[4096,256]{0,1:T(8,128)}, u32[]{:S(2)}) copy-start(f32[4096,256]{0,1:T(8,128)} %get-tuple-element.103) | copy-start | bytes 12582916
Sparse Core Ops, SparseCore 0:
  287.9 48.1 all-reduce.22
  383.4 175.5 all-reduce.14
  593.9 103.7 all-reduce.20
  777.9 45.4 all-reduce.18
  867.1 175.5 all-reduce.12
  1077.4 103.7 all-reduce.16
where the time goes:
time: 1350 us; the launch traced here: 1340 us
  waiting for transfers between devices  622 us (46%)
  other arithmetic  292 us (22%)
  local copies, waits for them, and re-layouts  246 us (18%)
  matrix products  165 us (12%)
  between operations  14.1 us (1%)
    psum x4, waiting for transfers between devices, spread(): return lax.psum(block, axis)  428 us
    psum x2, waiting for transfers between devices, on_device(): lax.psum((jnp.where(keeper, select_columns(got_half), 0.0), jnp.where(kee...  194 us
    unnamed x4, other arithmetic  187 us
    dot_general x6, matrix products, product_trans(): lax.dot_general(left, right, (((1,), (1,)), ((), ())), precision=highest,...  150 us
    unnamed x29, local copies, waits for them, and re-layouts  117 us
    reshape x1, local copies, waits for them, and re-layouts, on_device(): return local.reshape(row_tiles, 1, width, col_tiles, 1, width)  48.7 us
    another operation x5, other arithmetic, diagonal_core(): lax.linalg.triangular_solve(diag_factor, identity, left_side=True, lower=...  41.3 us
    reshape x1, local copies, waits for them, and re-layouts, on_device(): local = matrix.reshape(height, col_tiles * width)  31.1 us
  transfers between devices with their start and end apart: 6, of which 6 were waited for; matrix products, arithmetic and copies ran while one was open for 2% of the time, Pallas kernels for 0%

commit v1 on v0

v1 whole, which is shorter than its diff:
```python
import jax
import jax.numpy as jnp
from jax import lax
from jax.sharding import PartitionSpec as P

BLOCKS = 2
BASE = 16

highest = lax.Precision.HIGHEST
high = lax.Precision.HIGH


def product(left, right):
    return jnp.dot(left, right, precision=highest, preferred_element_type=jnp.float32)


def product_trans(left, right, precision=highest):
    return lax.dot_general(
        left, right, (((1,), (1,)), ((), ())), precision=precision, preferred_element_type=jnp.float32
    )


def batched(left, right):
    return jnp.einsum("bij,bjk->bik", left, right, precision=highest, preferred_element_type=jnp.float32)


def invert(lower):
    count, width, _ = lower.shape
    size = BASE if width % BASE == 0 else width

    def blocks(extent, row, col):
        return lower[:, row * extent : (row + 1) * extent, col * extent : (col + 1) * extent]

    parts = width // size
    diag = jnp.stack([blocks(size, i, i) for i in range(parts)], 1).reshape(count * parts, size, size)
    rows = jnp.arange(size)[None, :, None]
    result = jnp.broadcast_to(jnp.eye(size, dtype=jnp.float32), diag.shape)
    for i in range(size):
        pivot = result[:, i : i + 1, :] / diag[:, i : i + 1, i : i + 1]
        changed = jnp.where(rows > i, result - diag[:, :, i : i + 1] * pivot, result)
        result = lax.optimization_barrier(jnp.where(rows == i, pivot, changed))
    while parts > 1:
        pairs = parts // 2
        split = result.reshape(count * pairs, 2, size, size)
        upper, under = split[:, 0], split[:, 1]
        cross = jnp.stack([blocks(size, 2 * j + 1, 2 * j) for j in range(pairs)], 1)
        cross = cross.reshape(count * pairs, size, size)
        corner = -batched(batched(under, cross), upper)
        top = jnp.concatenate([upper, jnp.zeros_like(upper)], 2)
        result = jnp.concatenate([top, jnp.concatenate([corner, under], 2)], 1)
        parts, size = pairs, 2 * size
    return result.reshape(count, width, width)


def core_of(block, inverse):
    symmetric = block + block.T - jnp.diag(jnp.diagonal(block))
    inner = product_trans(product(inverse, symmetric), inverse)
    return 0.5 * (inner + inner.T)


def on_device(matrix, factor):
    row_tiles = matrix.shape[0]
    width = matrix.shape[2]
    col_tiles = matrix.shape[3]
    prow_count = lax.axis_size("prow")
    pcol_count = lax.axis_size("pcol")
    prow_index = lax.axis_index("prow")
    pcol_index = lax.axis_index("pcol")
    height = row_tiles * width
    breadth = col_tiles * width
    tile_rows = jnp.arange(row_tiles, dtype=jnp.int32) * prow_count + prow_index
    tile_cols = jnp.arange(col_tiles, dtype=jnp.int32) * pcol_count + pcol_index
    offsets = jnp.arange(width, dtype=jnp.int32)
    elem_rows = (tile_rows[:, None] * width + offsets[None, :]).reshape(height)
    elem_cols = (tile_cols[:, None] * width + offsets[None, :]).reshape(breadth)
    row_tile_of = jnp.repeat(tile_rows, width)[:, None]
    col_tile_of = jnp.repeat(tile_cols, width)[:, None]
    ratio = pcol_count // prow_count
    keeper = prow_index == pcol_index % prow_count

    raw = []
    for step in range(BLOCKS):
        place = step // pcol_count
        raw.append((matrix[:, 0, :, place, 0, :], factor[:, 0, :, place, 0, :]))

    wanted = []
    for tile in range(BLOCKS):
        for step in range(tile + 1):
            held = (prow_index == tile % prow_count) & (pcol_index == step % pcol_count)
            for source in raw[step]:
                wanted.append(jnp.where(held, source[tile // prow_count], 0.0))
    corners = lax.psum(jnp.stack(wanted), ("prow", "pcol"))
    corner = {}
    index = 0
    for tile in range(BLOCKS):
        for step in range(tile + 1):
            corner[tile, step] = (corners[index], corners[index + 1])
            index += 2

    def select_columns(panel):
        shaped = panel.reshape(col_tiles, ratio, width, width)
        return lax.dynamic_index_in_dim(shaped, pcol_index // prow_count, 1, keepdims=False)

    row_panels, col_panels = [], []
    for step in range(BLOCKS):
        owner = pcol_index == step % pcol_count
        got = lax.psum(tuple(jnp.where(owner, source, 0.0) for source in raw[step]), "pcol")
        row_panels.append(tuple(part.reshape(height, width) for part in got))
        picked = lax.psum(tuple(jnp.where(keeper, select_columns(part), 0.0) for part in got), "prow")
        col_panels.append(tuple(part.reshape(breadth, width) for part in picked))

    inverses = invert(jnp.stack([corner[step, step][1] for step in range(BLOCKS)]))

    cores = []
    tile_half = {}
    for step in range(BLOCKS):
        block = corner[step, step][0]
        for before in range(step):
            half, fact = tile_half[step, before]
            block = block - jnp.tril(product_trans(half, fact) + product_trans(fact, half))
        inverse = inverses[step]
        core = core_of(block, inverse)
        cores.append(core)
        for tile in range(step + 1, BLOCKS):
            piece, fact = corner[tile, step]
            for before in range(step):
                half_row, fact_row = tile_half[tile, before]
                half_col, fact_col = tile_half[step, before]
                piece = piece - product_trans(half_row, fact_col) - product_trans(fact_row, half_col)
            tile_half[tile, step] = (product_trans(piece, inverse) - 0.5 * product(fact, core), fact)

    def reduce_panels(panels, tile_of):
        halves, facts, finals = [], [], []
        for step in range(BLOCKS):
            panel, fact = panels[step]
            below = tile_of > step
            fact = jnp.where(below, fact, 0.0)
            for before in range(step):
                half_col, fact_col = tile_half[step, before]
                panel = panel - product_trans(
                    jnp.concatenate([halves[before], facts[before]], 1),
                    jnp.concatenate([fact_col, half_col], 1),
                )
            shared = product(fact, cores[step])
            half = jnp.where(below, product_trans(panel, inverses[step]), 0.0) - 0.5 * shared
            halves.append(half)
            facts.append(fact)
            finals.append(half - 0.5 * shared)
        return halves, facts, finals

    row_half, row_fact, finals = reduce_panels(row_panels, row_tile_of)
    col_half, col_fact, _ = reduce_panels(col_panels, col_tile_of)
    left = jnp.concatenate([part for pair in zip(row_half, row_fact) for part in pair], 1)
    right = jnp.concatenate([part for pair in zip(col_fact, col_half) for part in pair], 1)
    update = product_trans(left, right, high)
    local = matrix.reshape(height, breadth)
    local = local - jnp.where(elem_rows[:, None] >= elem_cols[None, :], update, 0.0)
    for step in range(BLOCKS):
        first = step // pcol_count * width
        current = local[:, first : first + width]
        diag_rows = jnp.tile(jnp.tril(cores[step]), (row_tiles, 1))
        column = jnp.where(row_tile_of == step, diag_rows, jnp.where(row_tile_of > step, finals[step], current))
        column = jnp.where(pcol_index == step % pcol_count, column, current)
        local = local.at[:, first : first + width].set(column)
    return local.reshape(row_tiles, 1, width, col_tiles, 1, width)


def solution(mesh):
    placed = P(None, "prow", None, None, "pcol", None)
    return jax.shard_map(on_device, mesh=mesh, in_specs=(placed, placed), out_specs=placed, check_vma=False)
```

time: 1350 us -> 884 us (0.65)
  waiting for transfers between devices: 622 us -> 376 us
  other arithmetic: 292 us -> 147 us
  matrix products: 165 us -> 119 us
  local copies, waits for them, and re-layouts: 246 us -> 220 us
    psum x6 -> x3, waiting for transfers between devices: 622 us -> 376 us  [the longest x1 278 us: on_device(): lax.psum(tuple((jnp.where(owner, source, 0.0) for source in raw[step])),...]
    unnamed x4 -> x23, other arithmetic: 187 us -> 95.9 us
    dot_general x6 -> x20, matrix products: 150 us -> 104 us  [the longest x12 102 us: product_trans(): lax.dot_general(left, right, (((1,), (1,)), ((), ())), precision=precisio...]
    another operation x6 -> x7, other arithmetic: 42 us -> 1.07 us  [the longest x5 41.3 us: diagonal_core(): lax.linalg.triangular_solve(diag_factor, identity, left_side=True, lower=...]
    select_n x9 -> x27, other arithmetic: 43.7 us -> 21.4 us  [the longest x1 12.9 us: on_device(): jnp.where(owner, source, 0.0)]
    reshape x5 -> x4, local copies, waits for them, and re-layouts: 58.3 us -> 43.1 us  [the longest x1 31.1 us: on_device(): local = matrix.reshape(height, breadth)]
    unnamed x29 -> x75, local copies, waits for them, and re-layouts: 117 us -> 106 us
  transfers between devices with their start and end apart: 6 -> 3, of which waited for: 6 -> 2; matrix products, arithmetic and copies ran while one was open for 2% -> 30% of each run, Pallas kernels for 0% -> 0%
where the time goes in v1:
time: 884 us; the launch traced here: 878 us
  waiting for transfers between devices  376 us (43%)
  local copies, waits for them, and re-layouts  220 us (25%)
  other arithmetic  147 us (17%)
  matrix products  119 us (13%)
  between operations  14.7 us (2%)
    psum x1, waiting for transfers between devices, on_device(): lax.psum(tuple((jnp.where(owner, source, 0.0) for source in raw[step])),...  278 us
    unnamed x75, local copies, waits for them, and re-layouts  106 us
    dot_general x12, matrix products, product_trans(): lax.dot_general(left, right, (((1,), (1,)), ((), ())), precision=precisio...  102 us
    psum x1, waiting for transfers between devices, on_device(): lax.psum(tuple((jnp.where(keeper, select_columns(part), 0.0) for part in...  98.7 us
    unnamed x23, other arithmetic  95.9 us
    reshape x1, local copies, waits for them, and re-layouts, on_device(): return local.reshape(row_tiles, 1, width, col_tiles, 1, width)  48.7 us
    reshape x1, local copies, waits for them, and re-layouts, on_device(): local = matrix.reshape(height, breadth)  31.1 us
    scatter x2, other arithmetic, on_device(): local = local.at[:, first:first + width].set(column)  22 us
  transfers between devices with their start and end apart: 3, of which 2 were waited for; matrix products, arithmetic and copies ran while one was open for 30% of the time, Pallas kernels for 0%

profile of v1, /device:TPU:0, one launch (start us, length us, event | category | flops | bytes accessed | tf_op | source)
XLA Modules:
  0.0 877.9 jit_solution(8016696733492530095)
XLA Ops:
  10.3 12.9 %broadcast_select_fusion.2 = (f32[16,1,256,1,1,256]{5,4,3,2,1,0:T(1,128)S(1)}, f32[16,1,256,1,1,256]{5,4,3,2,1,0:T(1,128)S(1)}, f32[16,1,256,1,1,256]{5,4,3,2,1,0:T(1,128)S(1)}, f32[16,1,256,1,1,256]{5,4,3,2,1,0:T(1,128)S(1)}) fusion(pred[]{:T(512)S(6)} %eq.189, f32[16,1,256,8,1,256]{5,4,3,2,1,0:T(1,128)} %param.7, pred[]{:T(512)S(6)} %eq.209, ...), kind=kLoop, calls=%fused_computation.23 | loop fusion | flops 4194304 | bytes 25165826 | tf_op jit(solution)/shard_map/jit(_where)/select_n | solution.py:107
  23.1 2.5 copy.139
  25.6 2.4 copy.140
  28.0 2.5 copy.141
  30.5 2.4 copy.142
  34.1 94.7 %reduce.9 = f32[16,256,8,256]{3,2,1,0:T(8,128)} reduce(f32[16,1,256,8,1,256]{5,4,3,2,1,0:T(1,128)} %param.6, f32[]{:T(128)} %constant.197), dimensions={1,4}, to_apply=%param.6.reduce_sub_computation | reduce | bytes 67108864 | tf_op args[0]
  128.8 30.1 %copy.119 = f32[512,8,8,256]{3,1,2,0:T(8,128)} copy(f32[512,8,8,256]{3,2,1,0:T(8,128)} %bitcast.373) | data formatting | bytes 67108864
  158.8 31.1 %copy.96 = f32[4096,2048]{0,1:T(8,128)} copy(f32[4096,2048]{1,0:T(8,128)} %bitcast.374) | data formatting | bytes 67108864 | tf_op jit(solution)/shard_map/reshape | solution.py:156
  193.6 2.0 slice_bitcast_fusion.4
  205.0 277.6 %all-reduce.12.cloned.1.call-done = (f32[16,256,256]{2,1,0:T(8,128)}, f32[16,256,256]{2,1,0:T(8,128)}, f32[16,256,256]{2,1,0:T(8,128)}, f32[16,256,256]{2,1,0:T(8,128)}) async-done(((f32[16,256,256]{2,1,0:T(8,128)}, f32[16,256,256]{2,1,0:T(8,128)}, f32[16,256,256]{2,1,0:T(8,128)}, f32[16,256,256]{2,1,0:T(8,128)}), (f32[16,256,256]{2,1,0:T(8,128)}, f32[16,256,256]{2,1,0:T(8,128)}, f32[16,256,256]{2,1,0:T(8,128)}, ...) | async-done | bytes 16777232 | tf_op jit(solution)/shard_map/psum | solution.py:107
  482.6 3.1 constant_dynamic-slice_fusion
  485.7 2.4 copy.117
  488.2 2.2 copy.125
  490.7 1.5 constant_dynamic-slice_fusion.3
  492.2 2.2 copy.114
  494.6 2.3 copy.122
  497.1 1.5 constant_dynamic-slice_fusion.2
  498.6 2.2 copy.115
  501.0 2.2 copy.123
  503.5 1.5 constant_dynamic-slice_fusion.1
  504.9 2.2 copy.116
  507.3 2.2 copy.124
  511.0 2.4 gather_fusion
  517.1 2.7 gather_fusion.1
  521.5 5.7 copy.126
  527.7 5.9 copy.127
  533.6 5.9 copy.98
  539.5 5.9 copy.97
  545.4 2.9 broadcast_select_fusion.5
  548.3 4.3 convolution_multiply_fusion.1
  553.1 4.3 convolution_multiply_fusion
  557.8 5.1 fusion.18
  562.9 14.3 %fusion.20 = f32[4096,256]{1,0:T(8,128)S(1)} fusion(f32[4096,256]{1,0:T(8,128)S(1)} %bitcast.395, f32[4096,256]{0,1:T(8,128)S(1)} %broadcast_select_fusion.5, f32[4096,256]{0,1:T(8,128)S(1)} %fusion.18, f32[256,256]{1,0:T(8,128)S(1)} %fusion.34, f32[256,256]{1,0:T(8,128)S(1)} %get-tuple-element.45), kind=kOutput, calls=%fused_computation.33 | convolution fusion | flops 6445727744 | bytes 17301504 | tf_op jit(solution)/shard_map/dot_general | solution.py:18
  577.3 5.9 fusion.19
  583.2 98.7 %all-reduce.14.cloned.1.call-done = (f32[2048,256]{0,1:T(8,128)}, f32[2048,256]{0,1:T(8,128)}, f32[2048,256]{0,1:T(8,128)}, f32[2048,256]{0,1:T(8,128)}) async-done(((f32[2048,256]{0,1:T(8,128)}, f32[2048,256]{0,1:T(8,128)}, f32[2048,256]{0,1:T(8,128)}, f32[2048,256]{0,1:T(8,128)}), (f32[2048,256]{0,1:T(8,128)}, f32[2048,256]{0,1:T(8,128)}, f32[2048,256]{0,1:T(8,128)}, ...) | async-done | bytes 8388624 | tf_op jit(solution)/shard_map/psum | solution.py:109
  681.9 2.0 broadcast_select_fusion.7
  684.1 2.0 convolution_select_fusion.3
  686.2 2.2 fusion.32
  688.4 3.9 fusion.28
  692.3 2.0 convolution_select_fusion.2
  694.5 2.4 fusion.31
  697.0 4.7 fusion.122
  701.7 1.6 copy-done.6
  703.3 66.9 %select_subtract_fusion = f32[4096,2048]{0,1:T(8,128)} fusion(f32[4096,2048]{0,1:T(8,128)} %copy.96, f32[4096,256]{0,1:T(8,128)} %copy-done.7, f32[4096,256]{0,1:T(8,128)} %fusion.19, f32[4096,256]{0,1:T(8,128)S(1)} %copy-done.4, f32[4096,256]{0,1:T(8,128)S(1)} %copy-done.6, s32[4096]{0:T(1024)S(1)} %bitcast.452, s32[2048]{0:T(1024)S(1)} %bitcast.453, ...), kind=kOutput, calls=%fused_computation.2 | convolution fusion | flops 51577356288 | bytes 92299264 | tf_op jit(solution)/shard_map/dot_general | solution.py:18
  770.3 13.0 %constant_dynamic-update-slice_fusion.24 = (f32[4096,2048]{0,1:T(8,128)}, f32[4096,256]{0,1:T(8,128)}) fusion(f32[4096,2048]{0,1:T(8,128)} %select_subtract_fusion, f32[4096,256]{0,1:T(8,128)} %bitcast.386, f32[4096,256]{0,1:T(8,128)} %copy-done.5, f32[4096,256]{0,1:T(8,128)} %copy-done.2, pred[4096]{0:T(1024)(128)(4,1)S(1)} %gt.185, ...), kind=kLoop, calls=%fused_computation.230 | loop fusion | flops 5242880 | bytes 25174528 | tf_op jit(solution)/shard_map/scatter | solution.py:164
  783.3 9.0 %fusion.23 = f32[4096,2048]{0,1:T(8,128)} fusion(f32[4096,2048]{0,1:T(8,128)} %get-tuple-element.37, f32[4096,256]{0,1:T(8,128)} %get-tuple-element.38, f32[4096,256]{0,1:T(8,128)} %bitcast.379, f32[4096,256]{0,1:T(8,128)} %fusion.19, f32[4096,256]{0,1:T(8,128)S(1)} %copy-done.1, pred[4096]{0:T(1024)(128)(4,1)S(1)} %copy-done.23, pred[]{:T(512)S(6)} %eq.209, ...), kind=kLoop, calls=%fused_computation.34 | loop fusion | flops 5242880 | bytes 20980224 | tf_op jit(solution)/shard_map/scatter | solution.py:164
  792.3 30.2 %copy.128 = f32[256,8,16,256]{3,2,1,0:T(8,128)} copy(f32[256,8,16,256]{3,1,2,0:T(8,128)} %bitcast.378) | data formatting | bytes 67108864
  822.4 48.7 %copy.92 = f32[16,1,256,8,1,256]{5,4,3,2,1,0:T(1,128)} copy(f32[16,1,256,8,1,256]{2,0,5,3,4,1:T(8,128)} %bitcast.375) | data formatting | bytes 67108864 | tf_op jit(solution)/shard_map/reshape | solution.py:165
  (226 shorter events, 27.0 us)
Async XLA Ops:
  6.5 187.1 %all-reduce.10.cloned.1.call-start = ((), (), s32[]{:S(2)}) async-start(), calls=%async_computation | async-start | bytes 3145728 | tf_op jit(solution)/shard_map/psum | solution.py:92
  9.0 1.1 copy-start.15
  10.2 472.4 %all-reduce.12.cloned.1.call-start = ((), (), s32[]{:S(2)}) async-start(), calls=%async_computation.1 | async-start | bytes 33554432 | tf_op jit(solution)/shard_map/psum | solution.py:107
  32.9 649.0 %all-reduce.14.cloned.1.call-start = ((), (), s32[]{:S(2)}) async-start(), calls=%async_computation.2 | async-start | bytes 16777216 | tf_op jit(solution)/shard_map/psum | solution.py:109
  488.1 2.7 copy-start.11
  494.4 2.7 copy-start.9
  500.8 2.7 copy-start.12
  509.5 0.9 copy-start.20
  509.5 1.0 copy-start.21
  509.5 1.3 copy-start.19
  509.5 4.5 copy-start.14
  548.3 14.6 %copy-start.3 = (f32[4096,256]{0,1:T(8,128)}, f32[4096,256]{0,1:T(8,128)S(1)}, u32[]{:S(2)}) copy-start(f32[4096,256]{0,1:T(8,128)S(1)} %broadcast_select_fusion.5) | copy-start | bytes 12582916
  548.3 4.3 copy-start.8
  552.6 4.9 copy-start.2
  553.1 4.4 copy-start.7
  553.1 4.7 copy-start.10
  557.5 19.8 %copy-start = (f32[4096,256]{0,1:T(8,128)}, f32[4096,256]{0,1:T(8,128)S(1)}, u32[]{:S(2)}) copy-start(f32[4096,256]{0,1:T(8,128)S(1)} %convolution_multiply_fusion) | copy-start | bytes 12582916
  557.8 5.1 copy-start.13
  562.9 14.4 %copy-start.5 = (f32[4096,256]{0,1:T(8,128)}, f32[4096,256]{0,1:T(8,128)S(1)}, u32[]{:S(2)}) copy-start(f32[4096,256]{0,1:T(8,128)S(1)} %fusion.18) | copy-start | bytes 12582916
  577.3 104.6 %copy-start.22 = (pred[2048]{0:T(1024)(128)(4,1)S(1)}, pred[2048]{0:T(1024)(128)(4,1)}, u32[]{:S(2)}) copy-start(pred[2048]{0:T(1024)(128)(4,1)} %gt.206) | copy-start | bytes 6148
  681.9 2.2 copy-start.17
  686.2 2.2 copy-start.16
  692.3 2.1 copy-start.18
  696.9 4.8 copy-start.4
  697.0 6.4 copy-start.6
  697.0 6.4 copy-start.25
  697.0 6.4 copy-start.26
  703.3 67.0 %copy-start.24 = (pred[4096]{0:T(1024)(128)(4,1)S(1)}, pred[4096]{0:T(1024)(128)(4,1)}, u32[]{:S(2)}) copy-start(pred[4096]{0:T(1024)(128)(4,1)} %eq.213) | copy-start | bytes 12292
  770.3 13.0 %copy-start.1 = (f32[4096,256]{0,1:T(8,128)S(1)}, f32[4096,256]{0,1:T(8,128)}, u32[]{:S(2)}) copy-start(f32[4096,256]{0,1:T(8,128)} %copy-done) | copy-start | bytes 12582916
  770.3 13.0 %copy-start.23 = (pred[4096]{0:T(1024)(128)(4,1)S(1)}, pred[4096]{0:T(1024)(128)(4,1)}, u32[]{:S(2)}) copy-start(pred[4096]{0:T(1024)(128)(4,1)} %eq.215) | copy-start | bytes 12292
Sparse Core Ops, SparseCore 0:
  12.6 135.3 all-reduce.9
  150.8 331.7 all-reduce.11
  509.7 172.1 all-reduce.13
